TPU v7x, 16 devices: a whole 2x2x2 slice. The times are simulated.
16 devices in a mesh: batch: 2 (over z), row: 8 (over y, x, core).
Axes of the slice: x: 2, y: 2, z: 2, core: 2. Of those that a mesh axis runs over, the one named last changes fastest.
Arguments:
- trans_mat: bfloat16 [32768, 16384], P(('batch', 'row')), parts along dimension 0
- teleport: float32 [32768, 256], P(('batch', 'row')), parts along dimension 0
- dangling: int32 [32768], P(('batch', 'row')), parts along dimension 0
- damping: float32 [8], replicated
- rank_init: float32 [32768, 256], P(('batch', 'row')), parts along dimension 0
Outputs:
- output: float32 [32768, 256], P(('batch', 'row')), parts along dimension 0
There are 2 independent parts. A program takes and returns all parts, laid end to end along the dimension named above; an argument that names none is the same for every part.
All inputs are finite; a program needn't handle non-finite values.
Results may differ from a plain program's by a relative error of at most 0.001.
Values are sent between devices in bfloat16 or wider.
A program may use at most 1 GiB of HBM per device.

v0:
```python
import jax
import jax.numpy as jnp
from jax import lax
from jax.sharding import PartitionSpec as P, NamedSharding


def solution(mesh):
    spec_rows = P(("batch", "row"), None)
    spec_vec = P(("batch", "row"))

    def local_sweeps(mat_rows, tele_rows, dang_rows, damping, start_rows):
        num_nodes = mat_rows.shape[1]
        dang_float = dang_rows.astype(jnp.float32)
        rank_rows = start_rows
        for sweep_idx in range(damping.shape[0]):
            gathered = lax.all_gather(rank_rows.astype(jnp.bfloat16), "row", axis=0, tiled=True)
            dang_mass = lax.psum(jnp.dot(dang_float, rank_rows, preferred_element_type=jnp.float32), "row")
            prod_rows = jnp.dot(mat_rows, gathered, preferred_element_type=jnp.float32)
            factor = damping[sweep_idx]
            rank_rows = factor * prod_rows + (1.0 - factor) * tele_rows + (factor / num_nodes) * dang_mass[None, :]
        return rank_rows

    sharded_fn = jax.shard_map(local_sweeps, mesh=mesh, in_specs=(spec_rows, spec_rows, spec_vec, P(None), spec_rows), out_specs=spec_rows, check_vma=False)
    return sharded_fn
```

profile of v0, /device:TPU:0, one launch (start us, length us, event | category | flops | bytes accessed | tf_op | source)
XLA Modules:
  0.0 663.6 jit_solution(7011761308345521816)
XLA Ops:
  6.5 2.8 convert_element_type.27
  11.7 15.6 %psum.56 = f32[256]{0:T(256)S(1)} all-reduce(f32[256]{0:T(256)S(1)} %bitcast.107), channel_id=1, replica_groups=mesh['batch'=2,'row'=8] {'row'}, use_global_device_ids=true, to_apply=%region_0.0 | all-reduce | flops 256 | bytes 2048 | tf_op jit(solution)/shard_map/psum | solution.py:17
  27.3 35.3 %all-gather.9.cloned.1.call-done = bf16[16384,256]{1,0:T(8,128)(2,1)} async-done(((bf16[2048,256]{1,0:T(8,128)(2,1)}), bf16[16384,256]{1,0:T(8,128)(2,1)}) %all-gather.9.cloned.1.call-update) | async-done | bytes 8388624 | tf_op jit(solution)/shard_map/all_gather | solution.py:16
  62.6 32.1 %fusion.8 = bf16[2048,256]{1,0:T(8,128)(2,1)} fusion(bf16[2048,16384]{1,0:T(8,128)(2,1)} %param.5, bf16[16384,256]{1,0:T(8,128)(2,1)} %all-gather.9.cloned.1.call-done, f32[2048,256]{1,0:T(8,128)} %param.6, f32[256]{0:T(256)S(1)} %broadcast_multiply_fusion.7, f32[]{:T(128)S(6)} %sub.24, f32[]{:T(128)} %bitcast.7), kind=kOutput, calls=%fused_computation.16 | convolution fusion | flops 17182490624 | bytes 78644232 | tf_op jit(solution)/shard_map/dot_general | solution.py:18
  96.0 1.8 copy.6
  98.1 13.4 %psum.57 = f32[256]{0:T(256)S(1)} all-reduce(f32[256]{0:T(256)S(1)} %bitcast.108), channel_id=1, replica_groups=mesh['batch'=2,'row'=8] {'row'}, use_global_device_ids=true, to_apply=%region_1.0 | all-reduce | flops 256 | bytes 2048 | tf_op jit(solution)/shard_map/psum | solution.py:17
  111.6 33.6 %all-gather.11.cloned.1.call-done = bf16[16384,256]{1,0:T(8,128)(2,1)} async-done(((bf16[2048,256]{1,0:T(8,128)(2,1)}), bf16[16384,256]{1,0:T(8,128)(2,1)}) %all-gather.11.cloned.1.call-update) | async-done | bytes 8388624 | tf_op jit(solution)/shard_map/all_gather | solution.py:16
  145.1 29.9 %fusion.10 = bf16[2048,256]{0,1:T(8,128)(2,1)} fusion(bf16[16384,256]{1,0:T(8,128)(2,1)} %all-gather.11.cloned.1.call-done, bf16[2048,16384]{1,0:T(8,128)(2,1)} %param.5, f32[2048,256]{0,1:T(8,128)} %copy.6, f32[256]{0:T(256)S(1)} %broadcast_multiply_fusion.6, f32[]{:T(128)S(6)} %sub.25, f32[]{:T(128)} %bitcast.6), kind=kOutput, calls=%fused_computation.18 | convolution fusion | flops 17182490624 | bytes 78644232 | tf_op jit(solution)/shard_map/dot_general | solution.py:18
  176.6 1.6 fusion.26
  178.2 13.6 %psum.58 = f32[256]{0:T(256)S(1)} all-reduce(f32[256]{0:T(256)S(1)} %bitcast.109), channel_id=1, replica_groups=mesh['batch'=2,'row'=8] {'row'}, use_global_device_ids=true, to_apply=%region_2.0 | all-reduce | flops 256 | bytes 2048 | tf_op jit(solution)/shard_map/psum | solution.py:17
  191.8 33.6 %all-gather.13.cloned.1.call-done = bf16[16384,256]{0,1:T(8,128)(2,1)} async-done(((bf16[2048,256]{0,1:T(8,128)(2,1)}), bf16[16384,256]{0,1:T(8,128)(2,1)}) %all-gather.13.cloned.1.call-update) | async-done | bytes 8388624 | tf_op jit(solution)/shard_map/all_gather | solution.py:16
  225.4 29.4 %fusion.12 = bf16[2048,256]{0,1:T(8,128)(2,1)} fusion(bf16[16384,256]{0,1:T(8,128)(2,1)} %all-gather.13.cloned.1.call-done, bf16[2048,16384]{1,0:T(8,128)(2,1)} %param.5, f32[2048,256]{0,1:T(8,128)S(1)} %copy-done.3, f32[256]{0:T(256)S(1)} %broadcast_multiply_fusion.5, f32[]{:T(128)S(6)} %sub.26, f32[]{:T(128)} %bitcast.5), kind=kOutput, calls=%fused_computation.20 | convolution fusion | flops 17182490624 | bytes 78644232 | tf_op jit(solution)/shard_map/dot_general | solution.py:18
  256.0 1.6 fusion.27
  257.6 13.4 %psum.59 = f32[256]{0:T(256)S(1)} all-reduce(f32[256]{0:T(256)S(1)} %bitcast.110), channel_id=1, replica_groups=mesh['batch'=2,'row'=8] {'row'}, use_global_device_ids=true, to_apply=%region_3.0 | all-reduce | flops 256 | bytes 2048 | tf_op jit(solution)/shard_map/psum | solution.py:17
  271.0 34.2 %all-gather.15.cloned.1.call-done = bf16[16384,256]{0,1:T(8,128)(2,1)} async-done(((bf16[2048,256]{0,1:T(8,128)(2,1)}), bf16[16384,256]{0,1:T(8,128)(2,1)}) %all-gather.15.cloned.1.call-update) | async-done | bytes 8388624 | tf_op jit(solution)/shard_map/all_gather | solution.py:16
  305.2 29.3 %fusion.14 = bf16[2048,256]{0,1:T(8,128)(2,1)} fusion(bf16[16384,256]{0,1:T(8,128)(2,1)} %all-gather.15.cloned.1.call-done, bf16[2048,16384]{1,0:T(8,128)(2,1)} %param.5, f32[2048,256]{0,1:T(8,128)S(1)} %copy-done.3, f32[256]{0:T(256)S(1)} %broadcast_multiply_fusion.4, f32[]{:T(128)S(6)} %sub.27, f32[]{:T(128)} %bitcast.4), kind=kOutput, calls=%fused_computation.22 | convolution fusion | flops 17182490624 | bytes 78644232 | tf_op jit(solution)/shard_map/dot_general | solution.py:18
  335.8 1.6 fusion.28
  337.4 13.4 %psum.60 = f32[256]{0:T(256)S(1)} all-reduce(f32[256]{0:T(256)S(1)} %bitcast.111), channel_id=1, replica_groups=mesh['batch'=2,'row'=8] {'row'}, use_global_device_ids=true, to_apply=%region_4.0 | all-reduce | flops 256 | bytes 2048 | tf_op jit(solution)/shard_map/psum | solution.py:17
  350.8 34.1 %all-gather.17.cloned.1.call-done = bf16[16384,256]{0,1:T(8,128)(2,1)} async-done(((bf16[2048,256]{0,1:T(8,128)(2,1)}), bf16[16384,256]{0,1:T(8,128)(2,1)}) %all-gather.17.cloned.1.call-update) | async-done | bytes 8388624 | tf_op jit(solution)/shard_map/all_gather | solution.py:16
  384.9 29.3 %fusion.16 = bf16[2048,256]{0,1:T(8,128)(2,1)} fusion(bf16[16384,256]{0,1:T(8,128)(2,1)} %all-gather.17.cloned.1.call-done, bf16[2048,16384]{1,0:T(8,128)(2,1)} %param.5, f32[2048,256]{0,1:T(8,128)S(1)} %copy-done.3, f32[256]{0:T(256)S(1)} %broadcast_multiply_fusion.3, f32[]{:T(128)S(6)} %sub.28, f32[]{:T(128)} %bitcast.3), kind=kOutput, calls=%fused_computation.24 | convolution fusion | flops 17182490624 | bytes 78644232 | tf_op jit(solution)/shard_map/dot_general | solution.py:18
  415.5 1.6 fusion.29
  417.1 13.7 %psum.61 = f32[256]{0:T(256)S(1)} all-reduce(f32[256]{0:T(256)S(1)} %bitcast.112), channel_id=1, replica_groups=mesh['batch'=2,'row'=8] {'row'}, use_global_device_ids=true, to_apply=%region_5.0 | all-reduce | flops 256 | bytes 2048 | tf_op jit(solution)/shard_map/psum | solution.py:17
  430.8 33.8 %all-gather.19.cloned.1.call-done = bf16[16384,256]{0,1:T(8,128)(2,1)} async-done(((bf16[2048,256]{0,1:T(8,128)(2,1)}), bf16[16384,256]{0,1:T(8,128)(2,1)}) %all-gather.19.cloned.1.call-update) | async-done | bytes 8388624 | tf_op jit(solution)/shard_map/all_gather | solution.py:16
  464.6 29.3 %fusion.18 = bf16[2048,256]{0,1:T(8,128)(2,1)} fusion(bf16[16384,256]{0,1:T(8,128)(2,1)} %all-gather.19.cloned.1.call-done, bf16[2048,16384]{1,0:T(8,128)(2,1)} %param.5, f32[2048,256]{0,1:T(8,128)S(1)} %copy-done.3, f32[256]{0:T(256)S(1)} %broadcast_multiply_fusion.2, f32[]{:T(128)S(6)} %sub.29, f32[]{:T(128)} %bitcast.2), kind=kOutput, calls=%fused_computation.26 | convolution fusion | flops 17182490624 | bytes 78644232 | tf_op jit(solution)/shard_map/dot_general | solution.py:18
  495.4 1.6 fusion.30
  497.0 13.4 %psum.62 = f32[256]{0:T(256)S(1)} all-reduce(f32[256]{0:T(256)S(1)} %bitcast.113), channel_id=1, replica_groups=mesh['batch'=2,'row'=8] {'row'}, use_global_device_ids=true, to_apply=%region_6.0 | all-reduce | flops 256 | bytes 2048 | tf_op jit(solution)/shard_map/psum | solution.py:17
  510.4 33.9 %all-gather.21.cloned.1.call-done = bf16[16384,256]{0,1:T(8,128)(2,1)} async-done(((bf16[2048,256]{0,1:T(8,128)(2,1)}), bf16[16384,256]{0,1:T(8,128)(2,1)}) %all-gather.21.cloned.1.call-update) | async-done | bytes 8388624 | tf_op jit(solution)/shard_map/all_gather | solution.py:16
  544.4 29.4 %fusion.20 = bf16[2048,256]{0,1:T(8,128)(2,1)} fusion(bf16[16384,256]{0,1:T(8,128)(2,1)} %all-gather.21.cloned.1.call-done, bf16[2048,16384]{1,0:T(8,128)(2,1)} %param.5, f32[2048,256]{0,1:T(8,128)S(1)} %copy-done.3, f32[256]{0:T(256)S(1)} %broadcast_multiply_fusion.1, f32[]{:T(128)S(6)} %sub.30, f32[]{:T(128)} %bitcast.1), kind=kOutput, calls=%fused_computation.28 | convolution fusion | flops 17182490624 | bytes 78644232 | tf_op jit(solution)/shard_map/dot_general | solution.py:18
  576.7 13.4 %psum.63 = f32[256]{0:T(256)S(1)} all-reduce(f32[256]{0:T(256)S(1)} %bitcast.106), channel_id=1, replica_groups=mesh['batch'=2,'row'=8] {'row'}, use_global_device_ids=true, to_apply=%region_7.0 | all-reduce | flops 256 | bytes 2048 | tf_op jit(solution)/shard_map/psum | solution.py:17
  590.2 34.0 %all-gather.23.cloned.1.call-done = bf16[16384,256]{0,1:T(8,128)(2,1)} async-done(((bf16[2048,256]{0,1:T(8,128)(2,1)}), bf16[16384,256]{0,1:T(8,128)(2,1)}) %all-gather.23.cloned.1.call-update) | async-done | bytes 8388624 | tf_op jit(solution)/shard_map/all_gather | solution.py:16
  624.2 29.7 %fusion.22 = f32[2048,256]{0,1:T(8,128)} fusion(bf16[16384,256]{0,1:T(8,128)(2,1)} %all-gather.23.cloned.1.call-done, bf16[2048,16384]{1,0:T(8,128)(2,1)} %param.5, f32[2048,256]{0,1:T(8,128)S(1)} %copy-done.3, f32[256]{0:T(256)S(1)} %broadcast_multiply_fusion, f32[]{:T(128)S(6)} %sub.31, f32[]{:T(128)} %bitcast), kind=kOutput, calls=%fused_computation.30 | convolution fusion | flops 17181966336 | bytes 79692808 | tf_op jit(solution)/shard_map/dot_general | solution.py:18
  653.9 2.9 copy.13
  (41 shorter events, 3.3 us)
Async XLA Ops:
  6.5 4.9 copy-start
  6.5 2.9 copy-start.5
  6.5 2.9 copy-start.4
  6.5 56.1 %all-gather.9.cloned.1.call-start = ((), (), s32[]{:S(2)}) async-start(), calls=%async_computation | async-start | bytes 9437184 | tf_op jit(solution)/shard_map/all_gather | solution.py:16
  9.4 135.7 %all-gather.11.cloned.1.call-start = ((), (), s32[]{:S(2)}) async-start(), calls=%async_computation.1 | async-start | bytes 9437184 | tf_op jit(solution)/shard_map/all_gather | solution.py:16
  62.6 33.4 %copy-start.2 = (f32[2048,256]{1,0:T(8,128)S(1)}, f32[2048,256]{1,0:T(8,128)}, u32[]{:S(2)}) copy-start(f32[2048,256]{1,0:T(8,128)} %param.6) | copy-start | bytes 6291460
  94.7 130.7 %all-gather.13.cloned.1.call-start = ((), (), s32[]{:S(2)}) async-start(), calls=%async_computation.2 | async-start | bytes 9437184 | tf_op jit(solution)/shard_map/all_gather | solution.py:16
  96.0 1.8 copy-start.1
  175.0 50.4 %copy-start.3 = (f32[2048,256]{0,1:T(8,128)S(1)}, f32[2048,256]{0,1:T(8,128)}, u32[]{:S(2)}) copy-start(f32[2048,256]{0,1:T(8,128)} %copy.6) | copy-start | bytes 6291460
  175.0 130.2 %all-gather.15.cloned.1.call-start = ((), (), s32[]{:S(2)}) async-start(), calls=%async_computation.3 | async-start | bytes 9437184 | tf_op jit(solution)/shard_map/all_gather | solution.py:16
  254.8 130.1 %all-gather.17.cloned.1.call-start = ((), (), s32[]{:S(2)}) async-start(), calls=%async_computation.4 | async-start | bytes 9437184 | tf_op jit(solution)/shard_map/all_gather | solution.py:16
  334.5 130.1 %all-gather.19.cloned.1.call-start = ((), (), s32[]{:S(2)}) async-start(), calls=%async_computation.5 | async-start | bytes 9437184 | tf_op jit(solution)/shard_map/all_gather | solution.py:16
  414.2 130.1 %all-gather.21.cloned.1.call-start = ((), (), s32[]{:S(2)}) async-start(), calls=%async_computation.6 | async-start | bytes 9437184 | tf_op jit(solution)/shard_map/all_gather | solution.py:16
  494.0 130.2 %all-gather.23.cloned.1.call-start = ((), (), s32[]{:S(2)}) async-start(), calls=%async_computation.7 | async-start | bytes 9437184 | tf_op jit(solution)/shard_map/all_gather | solution.py:16
Sparse Core Ops, SparseCore 0:
  9.5 53.0 all-gather.8
  94.9 50.2 all-gather.10
  175.2 50.2 all-gather.12
  254.9 50.2 all-gather.14
  334.6 50.2 all-gather.16
  414.3 50.2 all-gather.18
  494.1 50.2 all-gather.20
  573.9 50.2 all-gather.22
where the time goes:
time: 664 us
  waiting for transfers between devices  273 us (41%)
  matrix products  248 us (37%)
  blocking collectives  110 us (17%)
  between operations  23.9 us (4%)
    all_gather x8, waiting for transfers between devices, local_sweeps(): lax.all_gather(rank_rows.astype(jnp.bfloat16), 'row', axis=0, tiled=True)  272 us
    dot_general x8, matrix products, local_sweeps(): prod_rows = jnp.dot(mat_rows, gathered, preferred_element_type=jnp.float32)  238 us
    psum x8, blocking collectives, local_sweeps(): lax.psum(jnp.dot(dang_float, rank_rows, preferred_element_type=jnp.float3...  110 us
  transfers between devices with their start and end apart: 8, of which 8 were waited for; matrix products, arithmetic and copies ran while one was open for 2% of the time, Pallas kernels for 0%

commit v1 on v0

v1 whole, which is shorter than its diff:
```python
import functools

import jax
import jax.numpy as jnp
from jax import lax
from jax.experimental import pallas as pl
from jax.experimental.pallas import tpu as pltpu
from jax.sharding import PartitionSpec as P

MESH = pl.DeviceIdType.MESH
OWN, SIB, XN, XS, YN, YS, DG, DS = range(8)
X_OWN, Y_OWN, X_FWD, Y_FWD, S_OWN, S_X, S_Y, S_D = range(8)
RING = 12
UNITS = 24
KU = 512
KF = 256


def flip(a, b):
    return a + b - 2 * a * b


def kernel(num_sweeps, a_hbm, e_hbm, d_hbm, damp, r_hbm, out_hbm, g, ring, res, acc, ev, dcol, dbuf, mass,
           recv, send, mrecv, msend, ring_sem, res_sem, io_sem):
    rows = acc.shape[1]
    nodes = a_hbm.shape[1]
    group = lax.axis_index("batch")
    me = lax.axis_index("row")
    core = lax.rem(me, 2)
    xpos = lax.rem(lax.div(me, 2), 2)
    ypos = lax.div(me, 4)

    def index_of(sbit, xbit, ybit):
        return (flip(ypos, ybit) * 2 + flip(xpos, xbit)) * 2 + flip(core, sbit)

    def peer(slot):
        return (group, index_of(slot & 1, (slot >> 1) & 1, (slot >> 2) & 1))

    def remote(kind, p, h, c, src, dst):
        to = {X_OWN: XN, Y_OWN: YN, X_FWD: XN, Y_FWD: YN}.get(kind, SIB)
        return pltpu.make_async_remote_copy(src_ref=src, dst_ref=dst, send_sem=send.at[kind, p, h],
                                            recv_sem=recv.at[kind, p, h, c], device_id=peer(to), device_id_type=MESH)

    def block_copy(kind, p, h, c):
        src, dst = {X_OWN: (OWN, XN), Y_OWN: (OWN, YN), S_OWN: (OWN, SIB), S_X: (XN, XS), S_Y: (YN, YS),
                    S_D: (DG, DS)}[kind]
        at = pl.ds(pl.multiple_of(c * KU, KU), KU)
        return remote(kind, p, h, c, g.at[p, h, src, at], g.at[p, h, dst, at])

    def relay_copy(kind, p, h, f):
        src, start, part = (YN, 0, 0) if kind == X_FWD else (XN, rows // 2, KF)
        return remote(kind, p, h, f, g.at[p, h, src, pl.ds(start + f * KF, KF)],
                      g.at[p, h, DG, pl.ds(f * KU + part, KF)])

    def wait_relay(kind, p, h, f):
        part = 0 if kind == X_FWD else KF
        at = g.at[p, h, DG, pl.ds(pl.multiple_of(f * KU + part, KF), KF)]
        remote(kind, p, h, f, at, at).wait_recv()

    def wait_sends(p, h):
        for kind in range(8):
            size = rows // 2 if kind in (X_FWD, Y_FWD) else rows
            at = g.at[p, h, OWN, pl.ds(0, size)]
            remote(kind, p, h, 0, at, at).wait_send()

    def unit_copy(u):
        late = lax.div(lax.div(u, 8) + 1, 2)
        w = u - 8 * late
        early = 1 - late
        i = lax.rem(w, 4)
        j = lax.div(w, 4)
        sbit = early * j + late * lax.div(i, 2)
        ybit = late * lax.rem(i, 2)
        xbit = late * (1 - lax.rem(i, 2))
        part = early * i + late * j
        col = pl.multiple_of(index_of(sbit, xbit, ybit) * rows + part * KU, KU)
        slot = lax.rem(u, RING)
        return pltpu.make_async_copy(a_hbm.at[:, pl.ds(col, KU)], ring.at[slot], ring_sem.at[slot])

    def res_copy(i, f, part):
        col = pl.multiple_of(index_of(i, 1, 1) * rows + f * KF + part * (rows // 2), KF)
        return pltpu.make_async_copy(a_hbm.at[:, pl.ds(col, KF)], res.at[i, f, :, pl.ds(part * KF, KF)],
                                     res_sem.at[i, f, part])

    def half_copy(src, dst, h, sem):
        return pltpu.make_async_copy(src.at[:, pl.ds(h * 128, 128)], dst.at[h], sem)

    for h in range(2):
        half_copy(r_hbm, acc, h, io_sem.at[h]).start()
    d_copy = pltpu.make_async_copy(d_hbm, dbuf, io_sem.at[4])
    d_copy.start()

    @pl.loop(0, RING)
    def _(u):
        unit_copy(u).start()

    for h in range(2):
        half_copy(e_hbm, ev, h, io_sem.at[2 + h]).start()
    for i in range(2):
        for f in range(4):
            for part in range(2):
                res_copy(i, f, part).start()

    barrier = pltpu.get_barrier_semaphore()
    for slot in range(1, 8):
        pl.semaphore_signal(barrier, inc=1, device_id=peer(slot), device_id_type=MESH)
    pl.semaphore_wait(barrier, 7)

    def send_own(p, h, c):
        for kind in (X_OWN, Y_OWN, S_OWN):
            block_copy(kind, p, h, c).start()

    def mass_copy(p, h, slot):
        return pltpu.make_async_remote_copy(src_ref=mass.at[p, h, 0], dst_ref=mass.at[p, h, slot],
                                            send_sem=msend.at[p, h], recv_sem=mrecv.at[p, h, slot],
                                            device_id=peer(slot), device_id_type=MESH)

    def send_mass(p, h, part):
        mass[p, h, 0] = jnp.sum(part, axis=0, keepdims=True)
        for slot in range(1, 8):
            mass_copy(p, h, slot).start()

    def wait_mass_sends(p, h):
        at = mass.at[p, h, pl.ds(0, 7)]
        pltpu.make_async_remote_copy(src_ref=at, dst_ref=at, send_sem=msend.at[p, h], recv_sem=mrecv.at[p, h, 0],
                                     device_id=peer(SIB), device_id_type=MESH).wait_send()

    def fold(c, value):
        weighed = value * dcol[pl.ds(c * KU, KU), :]
        return jnp.sum(weighed.reshape(KU // 8, 8, 128), axis=0)

    for h in range(2):
        half_copy(r_hbm, acc, h, io_sem.at[h]).wait()
        for c in range(4):
            at = pl.ds(c * KU, KU)
            g[0, h, OWN, at] = acc[h, at].astype(jnp.bfloat16)
            if c:
                send_own(0, h, c - 1)
        send_own(0, h, 3)

    d_copy.wait()
    for c in range(rows // 128):
        line = jnp.broadcast_to(dbuf[pl.ds(c, 1), :].astype(jnp.float32), (128, 128))
        dcol[pl.ds(c * 128, 128), :] = line.T
    for h in range(2):
        part = jnp.zeros((8, 128), jnp.float32)
        for c in range(4):
            part += fold(c, acc[h, pl.ds(c * KU, KU)])
        send_mass(0, h, part)
        acc[h] = jnp.zeros_like(acc[h])

    for h in range(2):
        half_copy(e_hbm, ev, h, io_sem.at[2 + h]).wait()
    for i in range(2):
        for f in range(4):
            for part in range(2):
                res_copy(i, f, part).wait()

    def sweep(t, carry):
        p = lax.rem(t, 2)
        q = 1 - p
        more = t < num_sweeps - 1
        factor = damp[t]

        def wide(u, slot, c):
            unit_copy(u).wait()
            at = pl.ds(pl.multiple_of(c * KU, KU), KU)
            piece = jnp.concatenate([g[p, 0, slot, at], g[p, 1, slot, at]], axis=1)
            buf = ring.at[lax.rem(u, RING)]
            for m in range(rows // KU):
                mt = pl.ds(m * KU, KU)
                prod = jnp.dot(buf[mt], piece, preferred_element_type=jnp.float32)
                acc[0, mt] += prod[:, :128]
                acc[1, mt] += prod[:, 128:]

            @pl.when((u < RING) | more)
            def _():
                unit_copy(lax.rem(u + RING, UNITS)).start()

        @pl.loop(0, 4)
        def _(c):
            wide(c, OWN, c)

        @pl.loop(0, 4)
        def _(c):
            for h in range(2):
                block_copy(S_OWN, p, h, c).wait_recv()
            wide(c + 4, SIB, c)

        @pl.loop(0, 4)
        def _(c):
            for h in range(2):
                block_copy(X_OWN, p, h, c).wait_recv()
                block_copy(S_X, p, h, c).start()
                block_copy(Y_OWN, p, h, c).wait_recv()
                block_copy(S_Y, p, h, c).start()
                for kind, base in ((X_FWD, 0), (Y_FWD, 2)):
                    if h == 0:
                        for half in range(2):
                            @pl.when(c == base + half)
                            def _():
                                relay_copy(kind, p, 0, 2 * half).start()
                                relay_copy(kind, p, 0, 2 * half + 1).start()
                    else:
                        @pl.when(c == base + 1)
                        def _():
                            for f in range(4):
                                relay_copy(kind, p, 1, f).start()
            wide(4 * c + 8, XN, c)
            wide(4 * c + 9, YN, c)
            for h in range(2):
                block_copy(S_X, p, h, c).wait_recv()
            wide(4 * c + 10, XS, c)
            for h in range(2):
                block_copy(S_Y, p, h, c).wait_recv()
            wide(4 * c + 11, YS, c)

        @pl.loop(0, 2)
        def _(h):
            def narrow(i, f):
                at = pl.ds(pl.multiple_of(f * KU, KU), KU)
                piece = g[p, h, DG + i, at]
                for m in range(rows // KU):
                    mt = pl.ds(m * KU, KU)
                    acc[h, mt] += jnp.dot(res[i, f, mt], piece, preferred_element_type=jnp.float32)

            @pl.loop(0, 4)
            def _(f):
                wait_relay(X_FWD, p, h, f)
                wait_relay(Y_FWD, p, h, f)
                block_copy(S_D, p, h, f).start()

                @pl.when(f > 0)
                def _():
                    block_copy(S_D, p, h, f - 1).wait_recv()
                    narrow(1, f - 1)

                narrow(0, f)

            block_copy(S_D, p, h, 3).wait_recv()
            narrow(1, 3)

            for slot in range(1, 8):
                mass_copy(p, h, slot).wait_recv()
            line = (factor / nodes) * jnp.sum(mass[p, h], axis=0)

            def next_rows(c):
                at = pl.ds(c * KU, KU)
                return factor * acc[h, at] + (1.0 - factor) * ev[h, at] + line

            @pl.when(more)
            def _():
                part = jnp.zeros((8, 128), jnp.float32)
                for c in range(4):
                    at = pl.ds(c * KU, KU)
                    value = next_rows(c)
                    g[q, h, OWN, at] = value.astype(jnp.bfloat16)
                    part += fold(c, value)
                    acc[h, at] = jnp.zeros((KU, 128), jnp.float32)
                    if c:
                        send_own(q, h, c - 1)
                wait_sends(p, h)
                wait_mass_sends(p, h)
                send_own(q, h, 3)
                send_mass(q, h, part)

            @pl.when(jnp.logical_not(more))
            def _():
                for c in range(4):
                    acc[h, pl.ds(c * KU, KU)] = next_rows(c)
                pltpu.make_async_copy(acc.at[h], out_hbm.at[:, pl.ds(pl.multiple_of(h * 128, 128), 128)],
                                      io_sem.at[5 + h]).start()
                wait_sends(p, h)
                wait_mass_sends(p, h)

        return carry

    lax.fori_loop(0, num_sweeps, sweep, 0)
    for h in range(2):
        pltpu.make_async_copy(acc.at[h], out_hbm.at[:, pl.ds(h * 128, 128)], io_sem.at[5 + h]).wait()


def solution(mesh):
    spec_rows = P(("batch", "row"), None)
    spec_vec = P(("batch", "row"))

    def local_sweeps(mat_rows, tele_rows, dang_rows, damping, start_rows):
        rows, nodes = mat_rows.shape
        seeds = start_rows.shape[1]
        num_sweeps = damping.shape[0]
        any_space = pl.BlockSpec(memory_space=pl.ANY)
        sem = pltpu.SemaphoreType.DMA
        return pl.pallas_call(
            functools.partial(kernel, num_sweeps),
            out_shape=jax.ShapeDtypeStruct((rows, seeds), jnp.float32),
            in_specs=[any_space, any_space, any_space, pl.BlockSpec(memory_space=pltpu.SMEM), any_space],
            out_specs=any_space,
            scratch_shapes=[
                pltpu.VMEM((2, 2, 8, rows, 128), jnp.bfloat16),
                pltpu.VMEM((RING, rows, KU), jnp.bfloat16),
                pltpu.VMEM((2, 4, rows, KU), jnp.bfloat16),
                pltpu.VMEM((2, rows, 128), jnp.float32),
                pltpu.VMEM((2, rows, 128), jnp.float32),
                pltpu.VMEM((rows, 128), jnp.float32),
                pltpu.VMEM((rows // 128, 128), jnp.int32),
                pltpu.VMEM((2, 2, 8, 1, 128), jnp.float32),
                sem((8, 2, 2, 4)),
                sem((8, 2, 2)),
                sem((2, 2, 8)),
                sem((2, 2)),
                sem((RING,)),
                sem((2, 4, 2)),
                sem((7,)),
            ],
            compiler_params=pltpu.CompilerParams(collective_id=0, has_side_effects=True, vmem_limit_bytes=67043328),
            name="sweeps",
        )(mat_rows, tele_rows, dang_rows.reshape(rows // 128, 128), damping, start_rows)

    return jax.shard_map(local_sweeps, mesh=mesh, in_specs=(spec_rows, spec_rows, spec_vec, P(None), spec_rows),
                         out_specs=spec_rows, check_vma=False)
```

time: 664 us -> 291 us (0.44)
  Pallas kernels: 0 us -> 288 us
  waiting for transfers between devices: 273 us -> 0 us
  matrix products: 248 us -> 0 us
  blocking collectives: 110 us -> 0 us
  between operations: 23.9 us -> 0.01 us
    pallas_call x0 -> x1, Pallas kernels: none -> 288 us  [local_sweeps(): pl.pallas_call(functools.partial(kernel, num_sweeps), out_shape=jax.Shape...]
    all_gather x8 -> x0, waiting for transfers between devices: 272 us -> none  [local_sweeps(): lax.all_gather(rank_rows.astype(jnp.bfloat16), 'row', axis=0, tiled=True)]
    dot_general x16 -> x0, matrix products: 248 us -> none  [the longest x8 238 us: local_sweeps(): prod_rows = jnp.dot(mat_rows, gathered, preferred_element_type=jnp.float32)]
    psum x8 -> x0, blocking collectives: 110 us -> none  [local_sweeps(): lax.psum(jnp.dot(dang_float, rank_rows, preferred_element_type=jnp.float3...]
  transfers between devices with their start and end apart: 8 -> 0, of which waited for: 8 -> 0; matrix products, arithmetic and copies ran while one was open for 2% -> 0% of each run, Pallas kernels for 0% -> 0%
where the time goes in v1:
time: 291 us
  Pallas kernels  288 us (99%)
  local copies, waits for them, and re-layouts  3.05 us (1%)
    pallas_call x1, Pallas kernels, local_sweeps(): pl.pallas_call(functools.partial(kernel, num_sweeps), out_shape=jax.Shape...  288 us

profile of v1, /device:TPU:0, one launch (start us, length us, event | category | flops | bytes accessed | tf_op | source)
XLA Modules:
  0.0 290.9 jit_solution(17284740781912435706)
XLA Ops:
  0.0 287.8 %sweeps.1 = f32[2048,256]{1,0:T(8,128)} custom-call(bf16[2048,16384]{1,0:T(8,128)(2,1)} %a_hbm.1, f32[2048,256]{1,0:T(8,128)} %e_hbm.1, s32[16,128]{1,0:T(8,128)} %bitcast.1, f32[8]{0:T(128)} %damp.1, f32[2048,256]{1,0:T(8,128)} %r_hbm.1), custom_call_target="tpu_custom_call" | custom-call | tf_op jit(solution)/shard_map/sweeps/pallas_call | solution.py:293
  287.9 3.0 %copy.7 = f32[2048,256]{1,0:T(8,128)} copy(f32[2048,256]{1,0:T(8,128)} %sweeps.1) | data formatting | bytes 4194304

commit v2 on v1

v2 whole, which is shorter than its diff:
```python
import functools

import jax
import jax.numpy as jnp
from jax import lax
from jax.experimental import pallas as pl
from jax.experimental.pallas import tpu as pltpu
from jax.sharding import PartitionSpec as P

MESH = pl.DeviceIdType.MESH
OWN, SIB, XN, XS, YN, YS, DG, DS = range(8)
X_OWN, Y_OWN, X_FWD, Y_FWD, S_OWN, S_X, S_Y, S_D = range(8)
RING = 6
UNITS = 12
KU = 512
KF = 256
MB = 512
NEAR = (SIB, XN, YN)
KERNEL_VMEM = 64487424


def flip(a, b):
    return a + b - 2 * a * b


def kernel(num_sweeps, a_hbm, e_hbm, d_hbm, damp, r_hbm, acc, g, ring, res, ev, dcol, dbuf, mass,
           recv, send, mrecv, msend, ring_sem, res_sem, io_sem, ready):
    rows = acc.shape[1]
    nodes = a_hbm.shape[1]
    group = lax.axis_index("batch")
    me = lax.axis_index("row")
    core = lax.rem(me, 2)
    xpos = lax.rem(lax.div(me, 2), 2)
    ypos = lax.div(me, 4)

    def index_of(slot):
        sbit, xbit, ybit = slot & 1, (slot >> 1) & 1, (slot >> 2) & 1
        return (flip(ypos, ybit) * 2 + flip(xpos, xbit)) * 2 + flip(core, sbit)

    def peer(slot):
        return (group, index_of(slot))

    barrier = pltpu.get_barrier_semaphore()
    for slot in NEAR:
        pl.semaphore_signal(barrier, inc=1, device_id=peer(slot), device_id_type=MESH)

    def remote(kind, p, h, c, src, dst):
        to = {X_OWN: XN, Y_OWN: YN, X_FWD: XN, Y_FWD: YN}.get(kind, SIB)
        return pltpu.make_async_remote_copy(src_ref=src, dst_ref=dst, send_sem=send.at[kind, p, h],
                                            recv_sem=recv.at[kind, p, h, c], device_id=peer(to), device_id_type=MESH)

    def block_copy(kind, p, h, c):
        src, dst = {X_OWN: (OWN, XN), Y_OWN: (OWN, YN), S_OWN: (OWN, SIB), S_X: (XN, XS), S_Y: (YN, YS),
                    S_D: (DG, DS)}[kind]
        at = pl.ds(pl.multiple_of(c * KU, KU), KU)
        return remote(kind, p, h, c, g.at[p, h, src, at], g.at[p, h, dst, at])

    def relay_copy(kind, p, h, f):
        src, start, part = (YN, 0, 0) if kind == X_FWD else (XN, rows // 2, KF)
        return remote(kind, p, h, f, g.at[p, h, src, pl.ds(start + f * KF, KF)],
                      g.at[p, h, DG, pl.ds(f * KU + part, KF)])

    def wait_relay(kind, p, h, f):
        part = 0 if kind == X_FWD else KF
        at = g.at[p, h, DG, pl.ds(pl.multiple_of(f * KU + part, KF), KF)]
        remote(kind, p, h, f, at, at).wait_recv()

    def wait_sends(p, h):
        for kind in range(8):
            size = rows // 2 if kind in (X_FWD, Y_FWD) else rows
            at = g.at[p, h, OWN, pl.ds(0, size)]
            remote(kind, p, h, 0, at, at).wait_send()

    def parts_of(u):
        if u < 4:
            return [(u // 2, 2 * (u % 2)), (u // 2, 2 * (u % 2) + 1)]
        return [(slot, (u - 4) // 2) for slot in ((XN, YN) if u % 2 == 0 else (XS, YS))]

    def start_unit(u):
        parts = parts_of(u)
        if parts[0][0] == parts[1][0]:
            parts = [(parts[0][0], parts[0][1], 0, 2 * KU)]
        else:
            parts = [(slot, c, i * KU, KU) for i, (slot, c) in enumerate(parts)]
        for slot, c, to, size in parts:
            col = pl.multiple_of(index_of(slot) * rows + c * KU, KU)
            pltpu.make_async_copy(a_hbm.at[:, pl.ds(col, size)], ring.at[u % RING, :, pl.ds(to, size)],
                                  ring_sem.at[u % RING]).start()

    def wait_unit(u):
        at = ring.at[u % RING]
        pltpu.make_async_copy(at, at, ring_sem.at[u % RING]).wait()

    def res_copy(i, f, part):
        col = pl.multiple_of(index_of(DG + i) * rows + f * KF + part * (rows // 2), KF)
        return pltpu.make_async_copy(a_hbm.at[:, pl.ds(col, KF)], res.at[i, f, :, pl.ds(part * KF, KF)],
                                     res_sem.at[i, f, part])

    def half_copy(src, dst, h, sem):
        return pltpu.make_async_copy(src.at[:, pl.ds(h * 128, 128)], dst.at[h], sem)

    for h in range(2):
        half_copy(r_hbm, acc, h, io_sem.at[h]).start()
    d_copy = pltpu.make_async_copy(d_hbm, dbuf, io_sem.at[4])
    d_copy.start()
    pl.semaphore_wait(barrier, 3)

    def send_own(p, h, c):
        for kind in (X_OWN, Y_OWN, S_OWN):
            block_copy(kind, p, h, c).start()

    def mass_copy(p, h, slot):
        return pltpu.make_async_remote_copy(src_ref=mass.at[p, h, 0], dst_ref=mass.at[p, h, slot],
                                            send_sem=msend.at[p, h], recv_sem=mrecv.at[p, h, slot],
                                            device_id=peer(slot), device_id_type=MESH)

    def send_mass(p, h, part):
        mass[p, h, 0] = jnp.sum(part, axis=0, keepdims=True)
        for slot in range(1, 8):
            mass_copy(p, h, slot).start()

    def wait_mass_sends(p, h):
        at = mass.at[p, h, pl.ds(0, 7)]
        pltpu.make_async_remote_copy(src_ref=at, dst_ref=at, send_sem=msend.at[p, h], recv_sem=mrecv.at[p, h, 0],
                                     device_id=peer(SIB), device_id_type=MESH).wait_send()

    def fold(c, value):
        weighed = value * dcol[pl.ds(c * KU, KU), :]
        return jnp.sum(weighed.reshape(KU // 8, 8, 128), axis=0)

    for h in range(2):
        half_copy(r_hbm, acc, h, io_sem.at[h]).wait()
        for c in range(4):
            at = pl.ds(c * KU, KU)
            g[0, h, OWN, at] = acc[h, at].astype(jnp.bfloat16)
            if h == 0 and c in (1, 2):
                send_own(0, 0, c - 1)
    for h, c in ((1, 0), (1, 1), (0, 2), (1, 2), (0, 3), (1, 3)):
        send_own(0, h, c)

    for u in range(RING):
        start_unit(u)
    for h in range(2):
        half_copy(e_hbm, ev, h, io_sem.at[2 + h]).start()
    for i in range(2):
        for f in range(4):
            for part in range(2):
                res_copy(i, f, part).start()
    for slot in NEAR:
        pl.semaphore_signal(ready.at[0], inc=1, device_id=peer(slot), device_id_type=MESH)
    d_copy.wait()
    for c in range(rows // 128):
        line = jnp.broadcast_to(dbuf[pl.ds(c, 1), :].astype(jnp.float32), (128, 128))
        dcol[pl.ds(c * 128, 128), :] = line.T
    pl.semaphore_wait(ready.at[0], 3)
    for slot in NEAR:
        pl.semaphore_signal(ready.at[1], inc=1, device_id=peer(slot), device_id_type=MESH)
    sums = []
    for h in range(2):
        part = jnp.zeros((8, 128), jnp.float32)
        for c in range(4):
            part += fold(c, acc[h, pl.ds(c * KU, KU)])
        sums.append(part)
        acc[h] = jnp.zeros_like(acc[h])
    pl.semaphore_wait(ready.at[1], 3)
    for h in range(2):
        send_mass(0, h, sums[h])

    def sweep(t, carry):
        p = lax.rem(t, 2)
        q = 1 - p
        more = t < num_sweeps - 1
        factor = damp[t]

        def wide(u):
            wait_unit(u)
            piece = jnp.concatenate(
                [jnp.concatenate([g[p, h, slot, pl.ds(c * KU, KU)] for h in range(2)], axis=1) for slot, c in parts_of(u)],
                axis=0)
            for m in range(rows // MB):
                mt = pl.ds(m * MB, MB)
                prod = jnp.dot(ring[u % RING, mt], piece, preferred_element_type=jnp.float32)
                acc[0, mt] += prod[:, :128]
                acc[1, mt] += prod[:, 128:]
            if u + RING < UNITS:
                start_unit(u + RING)
            else:
                @pl.when(more)
                def _():
                    start_unit(u + RING - UNITS)

        wide(0)
        wide(1)
        for u in (2, 3):
            for slot, c in parts_of(u):
                for h in range(2):
                    block_copy(S_OWN, p, h, c).wait_recv()
            wide(u)
        for c in range(4):
            for h in range(2):
                block_copy(X_OWN, p, h, c).wait_recv()
                block_copy(S_X, p, h, c).start()
                block_copy(Y_OWN, p, h, c).wait_recv()
                block_copy(S_Y, p, h, c).start()
                kind = X_FWD if c < 2 else Y_FWD
                for f in ((2 * (c % 2), 2 * (c % 2) + 1) if h == 0 else range(4 * (c % 2))):
                    relay_copy(kind, p, h, f).start()
            wide(2 * c + 4)
            for h in range(2):
                block_copy(S_X, p, h, c).wait_recv()
                block_copy(S_Y, p, h, c).wait_recv()
            wide(2 * c + 5)

        @pl.when(t == 0)
        def _():
            for h in range(2):
                half_copy(e_hbm, ev, h, io_sem.at[2 + h]).wait()
            for i in range(2):
                for f in range(4):
                    for part in range(2):
                        res_copy(i, f, part).wait()

        for h in range(2):
            def narrow(*terms):
                pieces = [g[p, h, DG + i, pl.ds(pl.multiple_of(f * KU, KU), KU)] for i, f in terms]
                piece = jnp.concatenate(pieces, axis=0) if len(terms) > 1 else pieces[0]
                for m in range(rows // MB):
                    mt = pl.ds(m * MB, MB)
                    left = [res[i, f, mt] for i, f in terms]
                    left = jnp.concatenate(left, axis=1) if len(terms) > 1 else left[0]
                    acc[h, mt] += jnp.dot(left, piece, preferred_element_type=jnp.float32)

            def take(f):
                wait_relay(X_FWD, p, h, f)
                wait_relay(Y_FWD, p, h, f)
                block_copy(S_D, p, h, f).start()

            take(0)
            narrow((0, 0))

            @pl.loop(1, 4)
            def _(f):
                take(f)
                block_copy(S_D, p, h, f - 1).wait_recv()
                narrow((0, f), (1, f - 1))

            block_copy(S_D, p, h, 3).wait_recv()
            narrow((1, 3))

            for slot in range(1, 8):
                mass_copy(p, h, slot).wait_recv()
            line = (factor / nodes) * jnp.sum(mass[p, h], axis=0)

            def next_rows(c):
                at = pl.ds(c * KU, KU)
                return factor * acc[h, at] + (1.0 - factor) * ev[h, at] + line

            @pl.when(more)
            def _():
                part = jnp.zeros((8, 128), jnp.float32)
                for c in range(4):
                    at = pl.ds(c * KU, KU)
                    value = next_rows(c)
                    g[q, h, OWN, at] = value.astype(jnp.bfloat16)
                    part += fold(c, value)
                    acc[h, at] = jnp.zeros((KU, 128), jnp.float32)
                    if c in (1, 2):
                        send_own(q, h, c - 1)
                if h == 1:
                    send_own(q, 0, 2)
                    send_own(q, 1, 2)
                    for half in range(2):
                        wait_sends(p, half)
                        wait_mass_sends(p, half)
                    send_own(q, 0, 3)
                    send_own(q, 1, 3)
                send_mass(q, h, part)

            @pl.when(jnp.logical_not(more))
            def _():
                for c in range(4):
                    acc[h, pl.ds(c * KU, KU)] = next_rows(c)
                wait_sends(p, h)
                wait_mass_sends(p, h)

        return carry

    lax.fori_loop(0, num_sweeps, sweep, 0)


def finish(halves, out_hbm, sem):
    copies = [pltpu.make_async_copy(halves.at[h], out_hbm.at[:, pl.ds(h * 128, 128)], sem.at[h]) for h in range(2)]
    for copy in copies:
        copy.start()
    for copy in copies:
        copy.wait()


def solution(mesh):
    spec_rows = P(("batch", "row"), None)
    spec_vec = P(("batch", "row"))

    def local_sweeps(mat_rows, tele_rows, dang_rows, damping, start_rows):
        rows, nodes = mat_rows.shape
        seeds = start_rows.shape[1]
        num_sweeps = damping.shape[0]
        any_space = pl.BlockSpec(memory_space=pl.ANY)
        vmem = pl.BlockSpec(memory_space=pltpu.VMEM)
        sem = pltpu.SemaphoreType.DMA
        halves = pl.pallas_call(
            functools.partial(kernel, num_sweeps),
            out_shape=pltpu.VMEM((2, rows, 128), jnp.float32),
            in_specs=[any_space, any_space, any_space, pl.BlockSpec(memory_space=pltpu.SMEM), any_space],
            out_specs=vmem,
            scratch_shapes=[
                pltpu.VMEM((2, 2, 8, rows, 128), jnp.bfloat16),
                pltpu.VMEM((RING, rows, 2 * KU), jnp.bfloat16),
                pltpu.VMEM((2, 4, rows, KU), jnp.bfloat16),
                pltpu.VMEM((2, rows, 128), jnp.float32),
                pltpu.VMEM((rows, 128), jnp.float32),
                pltpu.VMEM((rows // 128, 128), jnp.int32),
                pltpu.VMEM((2, 2, 8, 1, 128), jnp.float32),
                sem((8, 2, 2, 4)),
                sem((8, 2, 2)),
                sem((2, 2, 8)),
                sem((2, 2)),
                sem((RING,)),
                sem((2, 4, 2)),
                sem((5,)),
                pltpu.SemaphoreType.REGULAR((2,)),
            ],
            compiler_params=pltpu.CompilerParams(collective_id=0, has_side_effects=True, vmem_limit_bytes=KERNEL_VMEM),
            name="sweeps",
        )(mat_rows, tele_rows, dang_rows.reshape(rows // 128, 128), damping, start_rows)
        return pl.pallas_call(
            finish,
            out_shape=jax.ShapeDtypeStruct((rows, seeds), jnp.float32),
            in_specs=[vmem],
            out_specs=any_space,
            scratch_shapes=[sem((2,))],
            compiler_params=pltpu.CompilerParams(vmem_limit_bytes=8 << 20),
            name="finish",
        )(halves)

    return jax.shard_map(local_sweeps, mesh=mesh, in_specs=(spec_rows, spec_rows, spec_vec, P(None), spec_rows),
                         out_specs=spec_rows, check_vma=False)
```

time: 291 us -> 284 us (0.976)
  Pallas kernels: 288 us -> 284 us
  local copies, waits for them, and re-layouts: 3.05 us -> 0 us
    pallas_call x1 -> x2, Pallas kernels: 288 us -> 284 us  [the longest x1 283 us: local_sweeps(): pl.pallas_call(functools.partial(kernel, num_sweeps), out_shape=pltpu.VME...]
    unnamed x1 -> x0, local copies, waits for them, and re-layouts: 3.05 us -> none
where the time goes in v2:
time: 284 us
  Pallas kernels  284 us (100%)
    pallas_call x1, Pallas kernels, local_sweeps(): pl.pallas_call(functools.partial(kernel, num_sweeps), out_shape=pltpu.VME...  283 us

profile of v2, /device:TPU:0, one launch (start us, length us, event | category | flops | bytes accessed | tf_op | source)
XLA Modules:
  0.0 284.4 jit_solution(14778108422099264164)
XLA Ops:
  0.0 283.0 %sweeps.1.halves = f32[2,2048,128]{2,1,0:T(8,128)S(1)} custom-call(bf16[2048,16384]{1,0:T(8,128)(2,1)} %a_hbm.1, f32[2048,256]{1,0:T(8,128)} %e_hbm.1, s32[16,128]{1,0:T(8,128)} %bitcast.1, f32[8]{0:T(128)} %damp.1, f32[2048,256]{1,0:T(8,128)} %r_hbm.1), custom_call_target="tpu_custom_call" | custom-call | tf_op jit(solution)/shard_map/sweeps/pallas_call | solution.py:310
  283.0 1.3 finish.1

commit v3 on v2

--- a/solution.py
+++ b/solution.py
@@ -24,7 +24,7 @@
 
 
 def kernel(num_sweeps, a_hbm, e_hbm, d_hbm, damp, r_hbm, acc, g, ring, res, ev, dcol, dbuf, mass,
-           recv, send, mrecv, msend, ring_sem, res_sem, io_sem, ready):
+           recv, send, mrecv, msend, ring_sem, res_sem, io_sem):
     rows = acc.shape[1]
     nodes = a_hbm.shape[1]
     group = lax.axis_index("batch")
@@ -105,24 +105,18 @@
     d_copy.start()
     pl.semaphore_wait(barrier, 3)
 
-    def send_own(p, h, c):
-        for kind in (X_OWN, Y_OWN, S_OWN):
+    def send_own(p, h, c, kinds=(X_OWN, Y_OWN, S_OWN)):
+        for kind in kinds:
             block_copy(kind, p, h, c).start()
 
-    def mass_copy(p, h, slot):
-        return pltpu.make_async_remote_copy(src_ref=mass.at[p, h, 0], dst_ref=mass.at[p, h, slot],
-                                            send_sem=msend.at[p, h], recv_sem=mrecv.at[p, h, slot],
-                                            device_id=peer(slot), device_id_type=MESH)
-
-    def send_mass(p, h, part):
-        mass[p, h, 0] = jnp.sum(part, axis=0, keepdims=True)
-        for slot in range(1, 8):
-            mass_copy(p, h, slot).start()
-
-    def wait_mass_sends(p, h):
-        at = mass.at[p, h, pl.ds(0, 7)]
-        pltpu.make_async_remote_copy(src_ref=at, dst_ref=at, send_sem=msend.at[p, h], recv_sem=mrecv.at[p, h, 0],
-                                     device_id=peer(SIB), device_id_type=MESH).wait_send()
+    def mass_copy(p, i):
+        return pltpu.make_async_remote_copy(src_ref=mass.at[p, i, 0], dst_ref=mass.at[p, i, 1],
+                                            send_sem=msend.at[p, i], recv_sem=mrecv.at[p, i],
+                                            device_id=peer(NEAR[i]), device_id_type=MESH)
+
+    def take_mass(p, i):
+        mass_copy(p, i).wait_recv()
+        mass[p, i + 1, 0] = mass[p, i, 0] + mass[p, i, 1]
 
     def fold(c, value):
         weighed = value * dcol[pl.ds(c * KU, KU), :]
@@ -135,8 +129,10 @@
             g[0, h, OWN, at] = acc[h, at].astype(jnp.bfloat16)
             if h == 0 and c in (1, 2):
                 send_own(0, 0, c - 1)
-    for h, c in ((1, 0), (1, 1), (0, 2), (1, 2), (0, 3), (1, 3)):
+    for h, c in ((1, 0), (1, 1)):
         send_own(0, h, c)
+    for h, c in ((0, 2), (1, 2), (0, 3), (1, 3)):
+        send_own(0, h, c, (S_OWN,))
 
     for u in range(RING):
         start_unit(u)
@@ -146,25 +142,17 @@
         for f in range(4):
             for part in range(2):
                 res_copy(i, f, part).start()
-    for slot in NEAR:
-        pl.semaphore_signal(ready.at[0], inc=1, device_id=peer(slot), device_id_type=MESH)
     d_copy.wait()
     for c in range(rows // 128):
         line = jnp.broadcast_to(dbuf[pl.ds(c, 1), :].astype(jnp.float32), (128, 128))
         dcol[pl.ds(c * 128, 128), :] = line.T
-    pl.semaphore_wait(ready.at[0], 3)
-    for slot in NEAR:
-        pl.semaphore_signal(ready.at[1], inc=1, device_id=peer(slot), device_id_type=MESH)
-    sums = []
     for h in range(2):
         part = jnp.zeros((8, 128), jnp.float32)
         for c in range(4):
             part += fold(c, acc[h, pl.ds(c * KU, KU)])
-        sums.append(part)
+        mass[0, 0, 0, :, h * 128:(h + 1) * 128] = jnp.sum(part, axis=0, keepdims=True)
         acc[h] = jnp.zeros_like(acc[h])
-    pl.semaphore_wait(ready.at[1], 3)
-    for h in range(2):
-        send_mass(0, h, sums[h])
+    mass_copy(0, 0).start()
 
     def sweep(t, carry):
         p = lax.rem(t, 2)
@@ -190,6 +178,12 @@
                     start_unit(u + RING - UNITS)
 
         wide(0)
+        take_mass(p, 0)
+        for h in range(2):
+            send_own(p, h, 2, (Y_OWN,))
+        mass_copy(p, 1).start()
+        for h, c, kind in ((0, 2, X_OWN), (1, 2, X_OWN), (0, 3, X_OWN), (0, 3, Y_OWN), (1, 3, X_OWN), (1, 3, Y_OWN)):
+            send_own(p, h, c, (kind,))
         wide(1)
         for u in (2, 3):
             for slot, c in parts_of(u):
@@ -203,9 +197,23 @@
                 block_copy(Y_OWN, p, h, c).wait_recv()
                 block_copy(S_Y, p, h, c).start()
                 kind = X_FWD if c < 2 else Y_FWD
-                for f in ((2 * (c % 2), 2 * (c % 2) + 1) if h == 0 else range(4 * (c % 2))):
-                    relay_copy(kind, p, h, f).start()
+                here = (2 * (c % 2), 2 * (c % 2) + 1)
+
+                @pl.when(more)
+                def _():
+                    for f in here if h == 0 else range(4 * (c % 2)):
+                        relay_copy(kind, p, h, f).start()
+
+                @pl.when(jnp.logical_not(more))
+                def _():
+                    for f in here if h == 1 else ():
+                        relay_copy(kind, p, 0, f).start()
+                        relay_copy(kind, p, 1, f).start()
+            if c == 1:
+                take_mass(p, 1)
             wide(2 * c + 4)
+            if c == 1:
+                mass_copy(p, 2).start()
             for h in range(2):
                 block_copy(S_X, p, h, c).wait_recv()
                 block_copy(S_Y, p, h, c).wait_recv()
@@ -220,68 +228,91 @@
                     for part in range(2):
                         res_copy(i, f, part).wait()
 
-        for h in range(2):
-            def narrow(*terms):
-                pieces = [g[p, h, DG + i, pl.ds(pl.multiple_of(f * KU, KU), KU)] for i, f in terms]
-                piece = jnp.concatenate(pieces, axis=0) if len(terms) > 1 else pieces[0]
-                for m in range(rows // MB):
-                    mt = pl.ds(m * MB, MB)
-                    left = [res[i, f, mt] for i, f in terms]
-                    left = jnp.concatenate(left, axis=1) if len(terms) > 1 else left[0]
-                    acc[h, mt] += jnp.dot(left, piece, preferred_element_type=jnp.float32)
-
-            def take(f):
-                wait_relay(X_FWD, p, h, f)
-                wait_relay(Y_FWD, p, h, f)
-                block_copy(S_D, p, h, f).start()
-
-            take(0)
-            narrow((0, 0))
-
-            @pl.loop(1, 4)
-            def _(f):
-                take(f)
-                block_copy(S_D, p, h, f - 1).wait_recv()
-                narrow((0, f), (1, f - 1))
-
-            block_copy(S_D, p, h, 3).wait_recv()
-            narrow((1, 3))
-
-            for slot in range(1, 8):
-                mass_copy(p, h, slot).wait_recv()
-            line = (factor / nodes) * jnp.sum(mass[p, h], axis=0)
-
-            def next_rows(c):
-                at = pl.ds(c * KU, KU)
-                return factor * acc[h, at] + (1.0 - factor) * ev[h, at] + line
-
-            @pl.when(more)
-            def _():
+        take_mass(p, 2)
+
+        def take(h, f):
+            wait_relay(X_FWD, p, h, f)
+            wait_relay(Y_FWD, p, h, f)
+            block_copy(S_D, p, h, f).start()
+
+        def right(h, i, f):
+            return g[p, h, DG + i, pl.ds(pl.multiple_of(f * KU, KU), KU)]
+
+        def next_rows(h, c):
+            at = pl.ds(c * KU, KU)
+            line = (factor / nodes) * mass[p, 3, 0, :, h * 128:(h + 1) * 128]
+            return factor * acc[h, at] + (1.0 - factor) * ev[h, at] + line
+
+        def wait_all_sends():
+            for h in range(2):
+                wait_sends(p, h)
+            for i in range(3):
+                mass_copy(p, i).wait_send()
+
+        @pl.when(more)
+        def _():
+            for h in range(2):
+                def narrow(*terms):
+                    pieces = [right(h, i, f) for i, f in terms]
+                    piece = jnp.concatenate(pieces, axis=0) if len(terms) > 1 else pieces[0]
+                    for m in range(rows // MB):
+                        mt = pl.ds(m * MB, MB)
+                        left = [res[i, f, mt] for i, f in terms]
+                        left = jnp.concatenate(left, axis=1) if len(terms) > 1 else left[0]
+                        acc[h, mt] += jnp.dot(left, piece, preferred_element_type=jnp.float32)
+
+                take(h, 0)
+                narrow((0, 0))
+
+                @pl.loop(1, 4)
+                def _(f):
+                    take(h, f)
+                    block_copy(S_D, p, h, f - 1).wait_recv()
+                    narrow((0, f), (1, f - 1))
+
+                block_copy(S_D, p, h, 3).wait_recv()
+                narrow((1, 3))
+
                 part = jnp.zeros((8, 128), jnp.float32)
                 for c in range(4):
                     at = pl.ds(c * KU, KU)
-                    value = next_rows(c)
+                    value = next_rows(h, c)
                     g[q, h, OWN, at] = value.astype(jnp.bfloat16)
                     part += fold(c, value)
                     acc[h, at] = jnp.zeros((KU, 128), jnp.float32)
                     if c in (1, 2):
                         send_own(q, h, c - 1)
-                if h == 1:
-                    send_own(q, 0, 2)
-                    send_own(q, 1, 2)
-                    for half in range(2):
-                        wait_sends(p, half)
-                        wait_mass_sends(p, half)
-                    send_own(q, 0, 3)
-                    send_own(q, 1, 3)
-                send_mass(q, h, part)
-
-            @pl.when(jnp.logical_not(more))
-            def _():
+                mass[q, 0, 0, :, h * 128:(h + 1) * 128] = jnp.sum(part, axis=0, keepdims=True)
+            for h in range(2):
+                send_own(q, h, 2, (S_OWN,))
+            mass_copy(q, 0).start()
+            wait_all_sends()
+            for h in range(2):
+                send_own(q, h, 3, (S_OWN,))
+
+        @pl.when(jnp.logical_not(more))
+        def _():
+            def both(i, f):
+                piece = jnp.concatenate([right(h, i, f) for h in range(2)], axis=1)
+                for m in range(rows // MB):
+                    mt = pl.ds(m * MB, MB)
+                    prod = jnp.dot(res[i, f, mt], piece, preferred_element_type=jnp.float32)
+                    acc[0, mt] += prod[:, :128]
+                    acc[1, mt] += prod[:, 128:]
+
+            @pl.loop(0, 4)
+            def _(f):
+                for h in range(2):
+                    take(h, f)
+                both(0, f)
+                for h in range(2):
+                    block_copy(S_D, p, h, f).wait_recv()
+                both(1, f)
+
+            for h in range(2):
                 for c in range(4):
-                    acc[h, pl.ds(c * KU, KU)] = next_rows(c)
-                wait_sends(p, h)
-                wait_mass_sends(p, h)
+                    acc[h, pl.ds(c * KU, KU)] = next_rows(h, c)
+            wait_all_sends()
 
         return carry
 
@@ -319,15 +350,14 @@
                 pltpu.VMEM((2, rows, 128), jnp.float32),
                 pltpu.VMEM((rows, 128), jnp.float32),
                 pltpu.VMEM((rows // 128, 128), jnp.int32),
-                pltpu.VMEM((2, 2, 8, 1, 128), jnp.float32),
+                pltpu.VMEM((2, 4, 2, 1, 256), jnp.float32),
                 sem((8, 2, 2, 4)),
                 sem((8, 2, 2)),
-                sem((2, 2, 8)),
-                sem((2, 2)),
+                sem((2, 3)),
+                sem((2, 3)),
                 sem((RING,)),
                 sem((2, 4, 2)),
                 sem((5,)),
-                pltpu.SemaphoreType.REGULAR((2,)),
             ],
             compiler_params=pltpu.CompilerParams(collective_id=0, has_side_effects=True, vmem_limit_bytes=KERNEL_VMEM),
             name="sweeps",

time: 284 us -> 281 us (0.989)
  Pallas kernels: 284 us -> 281 us
    pallas_call x1, Pallas kernels: 283 us -> 280 us  [local_sweeps(): pl.pallas_call(functools.partial(kernel, num_sweeps), out_shape=pltpu.VME...]
where the time goes in v3:
time: 281 us
  Pallas kernels  281 us (100%)
    pallas_call x1, Pallas kernels, local_sweeps(): pl.pallas_call(functools.partial(kernel, num_sweeps), out_shape=pltpu.VME...  280 us

profile of v3, /device:TPU:0, one launch (start us, length us, event | category | flops | bytes accessed | tf_op | source)
XLA Modules:
  0.0 281.3 jit_solution(4172333642262306166)
XLA Ops:
  0.0 280.0 %sweeps.1.halves = f32[2,2048,128]{2,1,0:T(8,128)S(1)} custom-call(bf16[2048,16384]{1,0:T(8,128)(2,1)} %a_hbm.1, f32[2048,256]{1,0:T(8,128)} %e_hbm.1, s32[16,128]{1,0:T(8,128)} %bitcast.1, f32[8]{0:T(128)} %damp.1, f32[2048,256]{1,0:T(8,128)} %r_hbm.1), custom_call_target="tpu_custom_call" | custom-call | tf_op jit(solution)/shard_map/sweeps/pallas_call | solution.py:341
  280.0 1.3 finish.1

commit v4 on v3

--- a/solution.py
+++ b/solution.py
@@ -24,7 +24,7 @@
 
 
 def kernel(num_sweeps, a_hbm, e_hbm, d_hbm, damp, r_hbm, acc, g, ring, res, ev, dcol, dbuf, mass,
-           recv, send, mrecv, msend, ring_sem, res_sem, io_sem):
+           near_sem, relay_sem, sib_sem, pass_sem, far_sem, send, mrecv, msend, ring_sem, res_sem, io_sem):
     rows = acc.shape[1]
     nodes = a_hbm.shape[1]
     group = lax.axis_index("batch")
@@ -44,10 +44,19 @@
     for slot in NEAR:
         pl.semaphore_signal(barrier, inc=1, device_id=peer(slot), device_id_type=MESH)
 
+    def arrival(kind, p, h, c):
+        if kind in (X_OWN, Y_OWN):
+            return near_sem.at[p, h, c]
+        if kind in (X_FWD, Y_FWD):
+            return relay_sem.at[h, c]
+        if kind == S_OWN:
+            return sib_sem.at[c // 2]
+        return far_sem.at[h, c] if kind == S_D else pass_sem.at[c]
+
     def remote(kind, p, h, c, src, dst):
         to = {X_OWN: XN, Y_OWN: YN, X_FWD: XN, Y_FWD: YN}.get(kind, SIB)
-        return pltpu.make_async_remote_copy(src_ref=src, dst_ref=dst, send_sem=send.at[kind, p, h],
-                                            recv_sem=recv.at[kind, p, h, c], device_id=peer(to), device_id_type=MESH)
+        return pltpu.make_async_remote_copy(src_ref=src, dst_ref=dst, send_sem=send.at[p, h],
+                                            recv_sem=arrival(kind, p, h, c), device_id=peer(to), device_id_type=MESH)
 
     def block_copy(kind, p, h, c):
         src, dst = {X_OWN: (OWN, XN), Y_OWN: (OWN, YN), S_OWN: (OWN, SIB), S_X: (XN, XS), S_Y: (YN, YS),
@@ -60,16 +69,25 @@
         return remote(kind, p, h, f, g.at[p, h, src, pl.ds(start + f * KF, KF)],
                       g.at[p, h, DG, pl.ds(f * KU + part, KF)])
 
-    def wait_relay(kind, p, h, f):
-        part = 0 if kind == X_FWD else KF
-        at = g.at[p, h, DG, pl.ds(pl.multiple_of(f * KU + part, KF), KF)]
-        remote(kind, p, h, f, at, at).wait_recv()
+    def wait_near(p, h, c):
+        at = g.at[p, h, pl.ds(0, 2), pl.ds(c * KU, KU)]
+        remote(X_OWN, p, h, c, at, at).wait_recv()
+
+    def wait_relays(p, h, f):
+        at = g.at[p, h, DG, pl.ds(pl.multiple_of(f * KU, KU), KU)]
+        remote(X_FWD, p, h, f, at, at).wait_recv()
+
+    def wait_sib(p, half):
+        at = g.at[p, :, SIB, pl.ds(half * 2 * KU, 2 * KU)]
+        remote(S_OWN, p, 0, 2 * half, at, at).wait_recv()
+
+    def wait_passed(p, c):
+        at = g.at[p, :, pl.ds(0, 2), pl.ds(c * KU, KU)]
+        remote(S_X, p, 0, c, at, at).wait_recv()
 
     def wait_sends(p, h):
-        for kind in range(8):
-            size = rows // 2 if kind in (X_FWD, Y_FWD) else rows
-            at = g.at[p, h, OWN, pl.ds(0, size)]
-            remote(kind, p, h, 0, at, at).wait_send()
+        at = g.at[p, h, pl.ds(0, 7)]
+        remote(S_D, p, h, 0, at, at).wait_send()
 
     def parts_of(u):
         if u < 4:
@@ -94,14 +112,14 @@
     def res_copy(i, f, part):
         col = pl.multiple_of(index_of(DG + i) * rows + f * KF + part * (rows // 2), KF)
         return pltpu.make_async_copy(a_hbm.at[:, pl.ds(col, KF)], res.at[i, f, :, pl.ds(part * KF, KF)],
-                                     res_sem.at[i, f, part])
+                                     res_sem.at[i, f // 2])
 
     def half_copy(src, dst, h, sem):
         return pltpu.make_async_copy(src.at[:, pl.ds(h * 128, 128)], dst.at[h], sem)
 
     for h in range(2):
         half_copy(r_hbm, acc, h, io_sem.at[h]).start()
-    d_copy = pltpu.make_async_copy(d_hbm, dbuf, io_sem.at[4])
+    d_copy = pltpu.make_async_copy(d_hbm, dbuf, io_sem.at[3])
     d_copy.start()
     pl.semaphore_wait(barrier, 3)
 
@@ -111,7 +129,7 @@
 
     def mass_copy(p, i):
         return pltpu.make_async_remote_copy(src_ref=mass.at[p, i, 0], dst_ref=mass.at[p, i, 1],
-                                            send_sem=msend.at[p, i], recv_sem=mrecv.at[p, i],
+                                            send_sem=msend.at[p], recv_sem=mrecv.at[p, i],
                                             device_id=peer(NEAR[i]), device_id_type=MESH)
 
     def take_mass(p, i):
@@ -137,7 +155,7 @@
     for u in range(RING):
         start_unit(u)
     for h in range(2):
-        half_copy(e_hbm, ev, h, io_sem.at[2 + h]).start()
+        half_copy(e_hbm, ev, h, io_sem.at[2]).start()
     for i in range(2):
         for f in range(4):
             for part in range(2):
@@ -186,15 +204,12 @@
             send_own(p, h, c, (kind,))
         wide(1)
         for u in (2, 3):
-            for slot, c in parts_of(u):
-                for h in range(2):
-                    block_copy(S_OWN, p, h, c).wait_recv()
+            wait_sib(p, u - 2)
             wide(u)
         for c in range(4):
             for h in range(2):
-                block_copy(X_OWN, p, h, c).wait_recv()
+                wait_near(p, h, c)
                 block_copy(S_X, p, h, c).start()
-                block_copy(Y_OWN, p, h, c).wait_recv()
                 block_copy(S_Y, p, h, c).start()
                 kind = X_FWD if c < 2 else Y_FWD
                 here = (2 * (c % 2), 2 * (c % 2) + 1)
@@ -214,25 +229,21 @@
             wide(2 * c + 4)
             if c == 1:
                 mass_copy(p, 2).start()
-            for h in range(2):
-                block_copy(S_X, p, h, c).wait_recv()
-                block_copy(S_Y, p, h, c).wait_recv()
+            wait_passed(p, c)
             wide(2 * c + 5)
 
         @pl.when(t == 0)
         def _():
-            for h in range(2):
-                half_copy(e_hbm, ev, h, io_sem.at[2 + h]).wait()
+            pltpu.make_async_copy(ev, ev, io_sem.at[2]).wait()
             for i in range(2):
-                for f in range(4):
-                    for part in range(2):
-                        res_copy(i, f, part).wait()
+                for half in range(2):
+                    at = res.at[i, pl.ds(2 * half, 2)]
+                    pltpu.make_async_copy(at, at, res_sem.at[i, half]).wait()
 
         take_mass(p, 2)
 
         def take(h, f):
-            wait_relay(X_FWD, p, h, f)
-            wait_relay(Y_FWD, p, h, f)
+            wait_relays(p, h, f)
             block_copy(S_D, p, h, f).start()
 
         def right(h, i, f):
@@ -246,8 +257,9 @@
         def wait_all_sends():
             for h in range(2):
                 wait_sends(p, h)
-            for i in range(3):
-                mass_copy(p, i).wait_send()
+            at = mass.at[p, pl.ds(0, 3), 0]
+            pltpu.make_async_remote_copy(src_ref=at, dst_ref=at, send_sem=msend.at[p], recv_sem=mrecv.at[p, 0],
+                                         device_id=peer(SIB), device_id_type=MESH).wait_send()
 
         @pl.when(more)
         def _():
@@ -292,26 +304,38 @@
 
         @pl.when(jnp.logical_not(more))
         def _():
-            def both(i, f):
+            def both(i, f, scale=None):
                 piece = jnp.concatenate([right(h, i, f) for h in range(2)], axis=1)
                 for m in range(rows // MB):
                     mt = pl.ds(m * MB, MB)
                     prod = jnp.dot(res[i, f, mt], piece, preferred_element_type=jnp.float32)
+                    if scale is not None:
+                        prod = scale * prod
                     acc[0, mt] += prod[:, :128]
                     acc[1, mt] += prod[:, 128:]
 
-            @pl.loop(0, 4)
-            def _(f):
+            def take_both(f):
                 for h in range(2):
                     take(h, f)
-                both(0, f)
+
+            def wait_far(f):
                 for h in range(2):
                     block_copy(S_D, p, h, f).wait_recv()
+
+            @pl.loop(0, 3)
+            def _(f):
+                take_both(f)
+                both(0, f)
+                wait_far(f)
                 both(1, f)
 
             for h in range(2):
                 for c in range(4):
                     acc[h, pl.ds(c * KU, KU)] = next_rows(h, c)
+            take_both(3)
+            both(0, 3, factor)
+            wait_far(3)
+            both(1, 3, factor)
             wait_all_sends()
 
         return carry
@@ -351,13 +375,17 @@
                 pltpu.VMEM((rows, 128), jnp.float32),
                 pltpu.VMEM((rows // 128, 128), jnp.int32),
                 pltpu.VMEM((2, 4, 2, 1, 256), jnp.float32),
-                sem((8, 2, 2, 4)),
-                sem((8, 2, 2)),
+                sem((2, 2, 4)),
+                sem((2, 4)),
+                sem((2,)),
+                sem((4,)),
+                sem((2, 4)),
+                sem((2, 2)),
                 sem((2, 3)),
-                sem((2, 3)),
+                sem((2,)),
                 sem((RING,)),
-                sem((2, 4, 2)),
-                sem((5,)),
+                sem((2, 2)),
+                sem((4,)),
             ],
             compiler_params=pltpu.CompilerParams(collective_id=0, has_side_effects=True, vmem_limit_bytes=KERNEL_VMEM),
             name="sweeps",

time: 281 us -> 280 us (level)
  no operation moved by 1% of the time
where the time goes in v4:
time: 280 us
  Pallas kernels  280 us (100%)
    pallas_call x1, Pallas kernels, local_sweeps(): pl.pallas_call(functools.partial(kernel, num_sweeps), out_shape=pltpu.VME...  279 us

profile of v4, /device:TPU:0, one launch (start us, length us, event | category | flops | bytes accessed | tf_op | source)
XLA Modules:
  0.0 280.0 jit_solution(7010447871617620808)
XLA Ops:
  0.0 278.6 %sweeps.1.halves = f32[2,2048,128]{2,1,0:T(8,128)S(1)} custom-call(bf16[2048,16384]{1,0:T(8,128)(2,1)} %a_hbm.1, f32[2048,256]{1,0:T(8,128)} %e_hbm.1, s32[16,128]{1,0:T(8,128)} %bitcast.1, f32[8]{0:T(128)} %damp.1, f32[2048,256]{1,0:T(8,128)} %r_hbm.1), custom_call_target="tpu_custom_call" | custom-call | tf_op jit(solution)/shard_map/sweeps/pallas_call | solution.py:365
  278.6 1.3 finish.1

commit v5 on v4

--- a/solution.py
+++ b/solution.py
@@ -23,7 +23,7 @@
     return a + b - 2 * a * b
 
 
-def kernel(num_sweeps, a_hbm, e_hbm, d_hbm, damp, r_hbm, acc, g, ring, res, ev, dcol, dbuf, mass,
+def kernel(num_sweeps, a_hbm, e_hbm, d_hbm, damp_hbm, r_hbm, acc, g, ring, res, ev, dcol, dbuf, damp, mass,
            near_sem, relay_sem, sib_sem, pass_sem, far_sem, send, mrecv, msend, ring_sem, res_sem, io_sem):
     rows = acc.shape[1]
     nodes = a_hbm.shape[1]
@@ -121,6 +121,8 @@
         half_copy(r_hbm, acc, h, io_sem.at[h]).start()
     d_copy = pltpu.make_async_copy(d_hbm, dbuf, io_sem.at[3])
     d_copy.start()
+    damp_copy = pltpu.make_async_copy(damp_hbm, damp, io_sem.at[4])
+    damp_copy.start()
     pl.semaphore_wait(barrier, 3)
 
     def send_own(p, h, c, kinds=(X_OWN, Y_OWN, S_OWN)):
@@ -171,6 +173,7 @@
         mass[0, 0, 0, :, h * 128:(h + 1) * 128] = jnp.sum(part, axis=0, keepdims=True)
         acc[h] = jnp.zeros_like(acc[h])
     mass_copy(0, 0).start()
+    damp_copy.wait()
 
     def sweep(t, carry):
         p = lax.rem(t, 2)
@@ -365,7 +368,7 @@
         halves = pl.pallas_call(
             functools.partial(kernel, num_sweeps),
             out_shape=pltpu.VMEM((2, rows, 128), jnp.float32),
-            in_specs=[any_space, any_space, any_space, pl.BlockSpec(memory_space=pltpu.SMEM), any_space],
+            in_specs=[any_space] * 5,
             out_specs=vmem,
             scratch_shapes=[
                 pltpu.VMEM((2, 2, 8, rows, 128), jnp.bfloat16),
@@ -374,6 +377,7 @@
                 pltpu.VMEM((2, rows, 128), jnp.float32),
                 pltpu.VMEM((rows, 128), jnp.float32),
                 pltpu.VMEM((rows // 128, 128), jnp.int32),
+                pltpu.SMEM(damping.shape, jnp.float32),
                 pltpu.VMEM((2, 4, 2, 1, 256), jnp.float32),
                 sem((2, 2, 4)),
                 sem((2, 4)),
@@ -385,7 +389,7 @@
                 sem((2,)),
                 sem((RING,)),
                 sem((2, 2)),
-                sem((4,)),
+                sem((5,)),
             ],
             compiler_params=pltpu.CompilerParams(collective_id=0, has_side_effects=True, vmem_limit_bytes=KERNEL_VMEM),
             name="sweeps",

time: 280 us -> 279 us (level)
  no operation moved by 1% of the time
where the time goes in v5:
time: 279 us
  Pallas kernels  279 us (100%)
    pallas_call x1, Pallas kernels, local_sweeps(): pl.pallas_call(functools.partial(kernel, num_sweeps), out_shape=pltpu.VME...  278 us

profile of v5, /device:TPU:0, one launch (start us, length us, event | category | flops | bytes accessed | tf_op | source)
XLA Modules:
  0.0 279.3 jit_solution(11545575391068218873)
XLA Ops:
  0.0 278.0 %sweeps.1.halves = f32[2,2048,128]{2,1,0:T(8,128)S(1)} custom-call(bf16[2048,16384]{1,0:T(8,128)(2,1)} %a_hbm.1, f32[2048,256]{1,0:T(8,128)} %e_hbm.1, s32[16,128]{1,0:T(8,128)} %bitcast.1, f32[8]{0:T(128)} %damp_hbm.1, f32[2048,256]{1,0:T(8,128)} %r_hbm.1), custom_call_target="tpu_custom_call" | custom-call | tf_op jit(solution)/shard_map/sweeps/pallas_call | solution.py:368
  278.0 1.3 finish.1

commit v6 on v5

--- a/solution.py
+++ b/solution.py
@@ -13,7 +13,8 @@
 RING = 6
 UNITS = 12
 KU = 512
-KF = 256
+FS = (384, 256, 256, 128)
+FO = (0, 384, 640, 896)
 MB = 512
 NEAR = (SIB, XN, YN)
 KERNEL_VMEM = 64487424
@@ -58,23 +59,26 @@
         return pltpu.make_async_remote_copy(src_ref=src, dst_ref=dst, send_sem=send.at[p, h],
                                             recv_sem=arrival(kind, p, h, c), device_id=peer(to), device_id_type=MESH)
 
+    def far_rows(f):
+        return pl.ds(2 * FO[f], 2 * FS[f])
+
     def block_copy(kind, p, h, c):
         src, dst = {X_OWN: (OWN, XN), Y_OWN: (OWN, YN), S_OWN: (OWN, SIB), S_X: (XN, XS), S_Y: (YN, YS),
                     S_D: (DG, DS)}[kind]
-        at = pl.ds(pl.multiple_of(c * KU, KU), KU)
+        at = far_rows(c) if kind == S_D else pl.ds(c * KU, KU)
         return remote(kind, p, h, c, g.at[p, h, src, at], g.at[p, h, dst, at])
 
     def relay_copy(kind, p, h, f):
-        src, start, part = (YN, 0, 0) if kind == X_FWD else (XN, rows // 2, KF)
-        return remote(kind, p, h, f, g.at[p, h, src, pl.ds(start + f * KF, KF)],
-                      g.at[p, h, DG, pl.ds(f * KU + part, KF)])
+        src, start, part = (YN, 0, 0) if kind == X_FWD else (XN, rows // 2, 1)
+        return remote(kind, p, h, f, g.at[p, h, src, pl.ds(start + FO[f], FS[f])],
+                      g.at[p, h, DG, pl.ds(2 * FO[f] + part * FS[f], FS[f])])
 
     def wait_near(p, h, c):
         at = g.at[p, h, pl.ds(0, 2), pl.ds(c * KU, KU)]
         remote(X_OWN, p, h, c, at, at).wait_recv()
 
     def wait_relays(p, h, f):
-        at = g.at[p, h, DG, pl.ds(pl.multiple_of(f * KU, KU), KU)]
+        at = g.at[p, h, DG, far_rows(f)]
         remote(X_FWD, p, h, f, at, at).wait_recv()
 
     def wait_sib(p, half):
@@ -110,9 +114,9 @@
         pltpu.make_async_copy(at, at, ring_sem.at[u % RING]).wait()
 
     def res_copy(i, f, part):
-        col = pl.multiple_of(index_of(DG + i) * rows + f * KF + part * (rows // 2), KF)
-        return pltpu.make_async_copy(a_hbm.at[:, pl.ds(col, KF)], res.at[i, f, :, pl.ds(part * KF, KF)],
-                                     res_sem.at[i, f // 2])
+        col = pl.multiple_of(index_of(DG + i) * rows + FO[f] + part * (rows // 2), 128)
+        return pltpu.make_async_copy(a_hbm.at[:, pl.ds(col, FS[f])],
+                                     res.at[i, :, pl.ds(2 * FO[f] + part * FS[f], FS[f])], res_sem.at[i])
 
     def half_copy(src, dst, h, sem):
         return pltpu.make_async_copy(src.at[:, pl.ds(h * 128, 128)], dst.at[h], sem)
@@ -215,7 +219,7 @@
                 block_copy(S_X, p, h, c).start()
                 block_copy(S_Y, p, h, c).start()
                 kind = X_FWD if c < 2 else Y_FWD
-                here = (2 * (c % 2), 2 * (c % 2) + 1)
+                here = (1, 2, 3) if c % 2 else (0,)
 
                 @pl.when(more)
                 def _():
@@ -239,9 +243,7 @@
         def _():
             pltpu.make_async_copy(ev, ev, io_sem.at[2]).wait()
             for i in range(2):
-                for half in range(2):
-                    at = res.at[i, pl.ds(2 * half, 2)]
-                    pltpu.make_async_copy(at, at, res_sem.at[i, half]).wait()
+                pltpu.make_async_copy(res.at[i], res.at[i], res_sem.at[i]).wait()
 
         take_mass(p, 2)
 
@@ -250,7 +252,7 @@
             block_copy(S_D, p, h, f).start()
 
         def right(h, i, f):
-            return g[p, h, DG + i, pl.ds(pl.multiple_of(f * KU, KU), KU)]
+            return g[p, h, DG + i, far_rows(f)]
 
         def next_rows(h, c):
             at = pl.ds(c * KU, KU)
@@ -272,15 +274,14 @@
                     piece = jnp.concatenate(pieces, axis=0) if len(terms) > 1 else pieces[0]
                     for m in range(rows // MB):
                         mt = pl.ds(m * MB, MB)
-                        left = [res[i, f, mt] for i, f in terms]
+                        left = [res[i, mt, far_rows(f)] for i, f in terms]
                         left = jnp.concatenate(left, axis=1) if len(terms) > 1 else left[0]
                         acc[h, mt] += jnp.dot(left, piece, preferred_element_type=jnp.float32)
 
                 take(h, 0)
                 narrow((0, 0))
 
-                @pl.loop(1, 4)
-                def _(f):
+                for f in range(1, 4):
                     take(h, f)
                     block_copy(S_D, p, h, f - 1).wait_recv()
                     narrow((0, f), (1, f - 1))
@@ -311,7 +312,7 @@
                 piece = jnp.concatenate([right(h, i, f) for h in range(2)], axis=1)
                 for m in range(rows // MB):
                     mt = pl.ds(m * MB, MB)
-                    prod = jnp.dot(res[i, f, mt], piece, preferred_element_type=jnp.float32)
+                    prod = jnp.dot(res[i, mt, far_rows(f)], piece, preferred_element_type=jnp.float32)
                     if scale is not None:
                         prod = scale * prod
                     acc[0, mt] += prod[:, :128]
@@ -325,8 +326,7 @@
                 for h in range(2):
                     block_copy(S_D, p, h, f).wait_recv()
 
-            @pl.loop(0, 3)
-            def _(f):
+            for f in range(3):
                 take_both(f)
                 both(0, f)
                 wait_far(f)
@@ -373,7 +373,7 @@
             scratch_shapes=[
                 pltpu.VMEM((2, 2, 8, rows, 128), jnp.bfloat16),
                 pltpu.VMEM((RING, rows, 2 * KU), jnp.bfloat16),
-                pltpu.VMEM((2, 4, rows, KU), jnp.bfloat16),
+                pltpu.VMEM((2, rows, rows), jnp.bfloat16),
                 pltpu.VMEM((2, rows, 128), jnp.float32),
                 pltpu.VMEM((rows, 128), jnp.float32),
                 pltpu.VMEM((rows // 128, 128), jnp.int32),
@@ -388,7 +388,7 @@
                 sem((2, 3)),
                 sem((2,)),
                 sem((RING,)),
-                sem((2, 2)),
+                sem((2,)),
                 sem((5,)),
             ],
             compiler_params=pltpu.CompilerParams(collective_id=0, has_side_effects=True, vmem_limit_bytes=KERNEL_VMEM),

time: 279 us -> 279 us (level)
  no operation moved by 1% of the time
where the time goes in v6:
time: 279 us
  Pallas kernels  279 us (100%)
    pallas_call x1, Pallas kernels, local_sweeps(): pl.pallas_call(functools.partial(kernel, num_sweeps), out_shape=pltpu.VME...  278 us

profile of v6, /device:TPU:0, one launch (start us, length us, event | category | flops | bytes accessed | tf_op | source)
XLA Modules:
  0.0 279.2 jit_solution(10281811020882982200)
XLA Ops:
  0.0 277.9 %sweeps.1.halves = f32[2,2048,128]{2,1,0:T(8,128)S(1)} custom-call(bf16[2048,16384]{1,0:T(8,128)(2,1)} %a_hbm.1, f32[2048,256]{1,0:T(8,128)} %e_hbm.1, s32[16,128]{1,0:T(8,128)} %bitcast.1, f32[8]{0:T(128)} %damp_hbm.1, f32[2048,256]{1,0:T(8,128)} %r_hbm.1), custom_call_target="tpu_custom_call" | custom-call | tf_op jit(solution)/shard_map/sweeps/pallas_call | solution.py:368
  277.9 1.3 finish.1
